TPU v7x, 16 devices: a 4x2x1 block of a 4x4x8 slice. The times are simulated.
16 devices in a mesh: rep: 4 (over y, z, core), dp: 4 (over x).
Axes of the slice: x: 4, y: 2, z: 1, core: 2. Of those that a mesh axis runs over, the one named last changes fastest.
The devices are a block of a 4x4x8 slice.
Arguments:
- x: bfloat16 [16, 4096, 640], P(('rep', 'dp')), parts along dimension 0
- dy: bfloat16 [16, 4096, 640], P(('rep', 'dp')), parts along dimension 0
- w_gate: bfloat16 [2, 640, 2048], replicated
- w_up: bfloat16 [2, 640, 2048], replicated
- w_down: bfloat16 [2, 2048, 640], replicated
- m_w_gate: float32 [2, 640, 2048], P(None, 'dp')
- m_w_up: float32 [2, 640, 2048], P(None, 'dp')
- m_w_down: float32 [2, 2048, 640], P(None, 'dp')
- v_w_gate: float32 [2, 640, 2048], P(None, 'dp')
- v_w_up: float32 [2, 640, 2048], P(None, 'dp')
- v_w_down: float32 [2, 2048, 640], P(None, 'dp')
Outputs:
- output 1: bfloat16 [8, 640, 2048], P('rep'), parts along dimension 0
- output 2: bfloat16 [8, 640, 2048], P('rep'), parts along dimension 0
- output 3: bfloat16 [8, 2048, 640], P('rep'), parts along dimension 0
- output 4: float32 [8, 640, 2048], P('rep', 'dp'), parts along dimension 0
- output 5: float32 [8, 640, 2048], P('rep', 'dp'), parts along dimension 0
- output 6: float32 [8, 2048, 640], P('rep', 'dp'), parts along dimension 0
- output 7: float32 [8, 640, 2048], P('rep', 'dp'), parts along dimension 0
- output 8: float32 [8, 640, 2048], P('rep', 'dp'), parts along dimension 0
- output 9: float32 [8, 2048, 640], P('rep', 'dp'), parts along dimension 0
There are 4 independent parts. A program takes and returns all parts, laid end to end along the dimension named above; an argument that names none is the same for every part.
All inputs are finite; a program needn't handle non-finite values.
Results may differ from a plain program's by a relative error of at most 0.022.
Values are sent between devices in bfloat16 or wider.
A program may use at most 768 MiB of HBM per device.

v0:
```python
import functools

import jax
import jax.numpy as jnp
from jax import lax
from jax.experimental import pallas as pl
from jax.experimental.pallas import tpu as pltpu
from jax.sharding import PartitionSpec as P


F32, BF16 = jnp.float32, jnp.bfloat16
VMEM_BYTES = 66_000_000
NN = (((1,), (0,)), ((), ()))
NT = (((1,), (1,)), ((), ()))


def dot(a, b, dims=NN):
    return lax.dot_general(a, b, dims, preferred_element_type=F32)


def params(**more):
    return pltpu.CompilerParams(vmem_limit_bytes=VMEM_BYTES, **more)


def cost(flops, nbytes):
    return pl.CostEstimate(flops=flops, bytes_accessed=nbytes, transcendentals=0)


def tokens_spec(tile, width):
    return pl.BlockSpec((tile, width), lambda i: (i, 0))


BLOCK = 512


def blocks_spec(tile, width):
    return pl.BlockSpec((width // BLOCK, tile, BLOCK), lambda i: (0, i, 0))


def blocks_shape(tokens, width):
    return jax.ShapeDtypeStruct((width // BLOCK, tokens, BLOCK), BF16)


def spread(hid_ref, which, hid):
    parts = hid_ref.shape[0]
    size = BLOCK // parts
    for j in range(parts):
        hid_ref[j, :, which * size : (which + 1) * size] = hid[:, j * size : (j + 1) * size]


def across_spec(tile, width):
    return pl.BlockSpec((width, tile), lambda i: (0, i))


def weight_spec(w, layer):
    return pl.BlockSpec((None, *w.shape[1:]), lambda i: (layer, 0, 0), pipeline_mode=pl.Buffered(1))


def scale_of(wide):
    return lax.rsqrt(jnp.mean(wide * wide, -1, keepdims=True) + 1e-6)


def gated(gate, up):
    sig = 0.5 * jnp.tanh(0.5 * gate) + 0.5
    act = gate * sig
    return act, up * (sig + act * (1.0 - sig)), (act * up).astype(BF16)


def front_kernel(x_ref, dy_ref, wg0, wu0, wd0, wg1, wu1, wd1, act_ref, slope_ref, hid0_ref, h1_ref, a0_ref, hid1_ref, dgate_ref, dup_ref, a1_ref, dy_out, whole_ref):
    wide = x_ref[...].astype(F32)
    a = (wide * scale_of(wide)).astype(BF16)
    a0_ref[...] = a.T
    for c in range(wg0.shape[1] // BLOCK):
        at = pl.ds(c * BLOCK, BLOCK)
        act, slope, hid = gated(dot(a, wg0[:, at]), dot(a, wu0[:, at]))
        act_ref[:, at] = act
        slope_ref[:, at] = slope
        whole_ref[:, at] = hid
        spread(hid0_ref, c, hid)
    y = dot(whole_ref[...], wd0[...]).astype(BF16)
    h = (wide + y.astype(F32)).astype(BF16)
    h1_ref[...] = h
    wide = h.astype(F32)
    a = (wide * scale_of(wide)).astype(BF16)
    a1_ref[...] = a.T
    dy = dy_ref[...]
    dy_out[...] = dy.T
    for c in range(wg1.shape[1] // BLOCK):
        at = pl.ds(c * BLOCK, BLOCK)
        act, slope, hid = gated(dot(a, wg1[:, at]), dot(a, wu1[:, at]))
        spread(hid1_ref, c, hid)
        dhid = dot(dy, wd1[at, :], NT).astype(BF16).astype(F32)
        dgate_ref[c] = (dhid * slope).astype(BF16)
        dup_ref[c] = (dhid * act).astype(BF16)


def front(x, dy, wg, wu, wd, tile=256):
    t, d = x.shape
    f = wg.shape[2]
    tokens, turned, wide = tokens_spec(tile, d), across_spec(tile, d), tokens_spec(tile, f)
    blocks = blocks_spec(tile, f)
    token_shape, turned_shape = jax.ShapeDtypeStruct((t, d), BF16), jax.ShapeDtypeStruct((d, t), BF16)
    wide_shape, block_shape = jax.ShapeDtypeStruct((t, f), F32), blocks_shape(t, f)
    return pl.pallas_call(
        front_kernel,
        grid=(t // tile,),
        in_specs=[tokens] * 2 + [weight_spec(w, layer) for layer in range(2) for w in (wg, wu, wd)],
        out_specs=[wide, wide, blocks, tokens, turned, blocks, blocks, blocks, turned, turned],
        out_shape=[wide_shape] * 2 + [block_shape, token_shape, turned_shape] + [block_shape] * 3 + [turned_shape] * 2,
        scratch_shapes=[pltpu.VMEM((tile, f), BF16)],
        compiler_params=pltpu.CompilerParams(vmem_limit_bytes=67_000_000),
        cost_estimate=cost(12 * t * d * f, 16 * t * f),
        name="front",
    )(x, dy, wg, wu, wd, wg, wu, wd)


N = 4


def back_kernel(axis, tile, rows_tile, *refs):
    (dy, dy_t, a1, hid1, dgate1, dup1, h1, act0, slope0, hid0, a0, wg, wu, wd), refs = refs[:14], refs[14:]
    (gd0, gd1, ggu0, ggu1, total_ref, dgate0, dup0), refs = refs[:7], refs[7:]
    a_buf, b_buf, wg_buf, wu_buf, wd_buf, dgate_buf, dup_buf, act_buf, slope_buf, h_buf, dy_buf, dgate_out, dup_out = refs[:13]
    term, got_l, got_r, sum_l, sum_r, stage, norms = refs[13:20]
    a_sem, b_sem, w_sem, tile_sem, out_sem, ready, norm_sem, send_sem, recv_sem = refs[20:]
    steps = hid1.shape[0]
    me = lax.axis_index(axis)
    right, left, across = ((me + k) % N for k in (1, 3, 2))
    mesh_id = pl.DeviceIdType.MESH

    def load_a(source, which, sem):
        return pltpu.make_async_copy(source, a_buf.at[which], a_sem.at[sem])

    def load_b(source, j, slot):
        return pltpu.make_async_copy(source.at[j], b_buf.at[slot], b_sem.at[slot])

    def start(copies):
        for one in copies:
            one.start()

    halves = ((across, 0), (right, 1), (across, 1), (left, 0), (right, 0), (left, 1), (me, 0), (me, 1))

    def put(kind, step, out):
        stage[kind][...] = (out.T if kind else out).astype(BF16)
        size = term[kind].shape[2]
        for place, (device, which) in enumerate(halves):
            rows = pl.ds(pl.multiple_of(device * 2 * size + which * size, 16), size)
            term[kind][step, place] = stage[kind][rows, :]

    def sends(kind, at, wanted):
        plan = (
            (pl.ds(0, 2), got_l, right),
            (pl.ds(2, 2), got_r, left),
            (4, sum_l, right),
            (5, sum_r, left),
        )
        s = at if kind else steps + at
        made = []
        for which in wanted:
            of, into, peer = plan[which]
            made.append(
                pltpu.make_async_remote_copy(
                    src_ref=term[kind].at[at, of],
                    dst_ref=into[kind].at[at],
                    send_sem=send_sem.at[which, s],
                    recv_sem=recv_sem.at[which, s],
                    device_id={axis: peer},
                    device_id_type=mesh_id,
                )
            )
        return made

    def pass_on(kind, at):
        arrived = sends(kind, at, (0, 1))
        onward = sends(kind, at, (2, 3))
        for one, then, place, got in ((arrived[0], onward[0], 4, got_l), (arrived[1], onward[1], 5, got_r)):
            one.wait_recv()
            term[kind][at, place] = (term[kind][at, place].astype(F32) + got[kind][at, 0].astype(F32)).astype(BF16)
            then.start()

    def finish(kind, at, gd, ggu):
        for one in sends(kind, at, (2, 3)):
            one.wait_recv()
        low = term[kind][at, 6].astype(F32) + sum_l[kind][at].astype(F32) + got_r[kind][at, 1].astype(F32)
        high = term[kind][at, 7].astype(F32) + got_l[kind][at, 1].astype(F32) + sum_r[kind][at].astype(F32)
        for which, g in enumerate((low, high)):
            g = g.astype(BF16)
            size = g.shape[0]
            if kind:
                gd[pl.ds(pl.multiple_of(at * 2 * size + which * size, size), size), :] = g
            else:
                columns = pl.ds(pl.multiple_of(at % steps * tile, tile), tile)
                ggu[at // steps, pl.ds(which * size, size), columns] = g
            square = g.astype(F32) * g.astype(F32)
            square = jnp.sum(square.reshape(-1, 8, square.shape[1]), 0)
            total_ref[...] += sum(square[:, c : c + 128] for c in range(0, square.shape[1], 128))

    def drain(kind, count):
        def one_step(at, _):
            for one in sends(kind, at, range(4)):
                one.wait_send()
            return 0

        lax.fori_loop(0, count, one_step, 0)

    def gradients(hid, dgate, dup, next_hid, before_first, gd, ggu):
        def down(j, _):
            slot = j % 2
            load_b(hid, j, slot).wait()
            put(1, j, dot(a_buf[0], b_buf[slot]))

            @pl.when(j < steps - 2)
            def _():
                load_b(hid, j + 2, slot).start()

            @pl.when(j >= steps - 2)
            def _():
                load_b(dgate, j + 2 - steps, slot).start()

            @pl.when(j == 0)
            def _():
                before_first()

            start(sends(1, j, (0, 1)))
            return 0

        lax.fori_loop(0, steps, down, 0)
        load_a(a1, 1, 1).wait()

        def gate_up(i, _):
            slot = i % 2
            load_b(dgate, i % steps, slot).wait()
            put(0, i, dot(a_buf[1], b_buf[slot]))

            @pl.when(i < steps - 2)
            def _():
                load_b(dgate, i + 2, slot).start()

            @pl.when((i >= steps - 2) & (i < 2 * steps - 2))
            def _():
                load_b(dup, i + 2 - steps, slot).start()

            if next_hid is not None:

                @pl.when(i >= 2 * steps - 2)
                def _():
                    load_b(next_hid, i + 2 - 2 * steps, slot).start()

            start(sends(0, i, (0, 1)))

            @pl.when(i < steps)
            def _():
                pass_on(1, i)

            @pl.when(i >= steps)
            def _():
                pass_on(0, i - steps)
                finish(1, i - steps, gd, ggu)

            return 0

        lax.fori_loop(0, 2 * steps, gate_up, 0)

    load_a(dy_t, 0, 0).start()
    load_b(hid1, 0, 0).start()
    load_b(hid1, 1, 1).start()
    load_a(a1, 1, 1).start()
    barrier = pltpu.get_barrier_semaphore()
    for peer in (right, left, across):
        pl.semaphore_signal(barrier, inc=1, device_id={axis: peer}, device_id_type=mesh_id)
    total_ref[...] = jnp.zeros_like(total_ref)
    weights = [
        pltpu.make_async_copy(wg.at[1], wg_buf, w_sem.at[0]),
        pltpu.make_async_copy(wu.at[1], wu_buf, w_sem.at[1]),
        pltpu.make_async_copy(wd.at[0], wd_buf, w_sem.at[2]),
    ]

    def tile_loads(i, slot):
        at = pl.ds(pl.multiple_of(i * rows_tile, rows_tile), rows_tile)
        blocks = [(one.at[:, at], buf) for one, buf in ((dgate1, dgate_buf), (dup1, dup_buf))]
        pairs = ((act0, act_buf), (slope0, slope_buf), (h1, h_buf), (dy, dy_buf))
        blocks += [(one.at[at], buf) for one, buf in pairs]
        return [pltpu.make_async_copy(a, b.at[slot], tile_sem.at[slot, k]) for k, (a, b) in enumerate(blocks)]

    def tile_stores(i, slot):
        at = pl.ds(pl.multiple_of(i * rows_tile, rows_tile), rows_tile)
        pairs = ((dgate_out, dgate0), (dup_out, dup0))
        return [pltpu.make_async_copy(a.at[slot], b.at[:, at], out_sem.at[slot, k]) for k, (a, b) in enumerate(pairs)]

    load_a(dy_t, 0, 0).wait()
    start(weights)
    start(tile_loads(0, 0))
    gradients(hid1, dgate1, dup1, hid0, lambda: pl.semaphore_wait(barrier, 3), gd1, ggu1)

    load_a(a0, 1, 1).start()
    for one in weights:
        one.wait()
    tiles = a_buf.shape[2] // rows_tile

    def tile_back(i, _):
        slot = i % 2
        at = pl.ds(pl.multiple_of(i * rows_tile, rows_tile), rows_tile)
        for one in tile_loads(i, slot):
            one.wait()

        @pl.when(i < tiles - 1)
        def _():
            start(tile_loads(i + 1, 1 - slot))

        @pl.when(i >= 2)
        def _():
            for one in tile_stores(i - 2, slot):
                one.wait()

        da = [
            sum(dot(w[:, c * tile : (c + 1) * tile], by[slot, c], NT) for c in range(steps)).astype(BF16)
            for w, by in ((wg_buf, dgate_buf), (wu_buf, dup_buf))
        ]
        da = da[0] + da[1]
        da = da.astype(F32).T
        wide = h_buf[slot].astype(F32)
        scale = scale_of(wide)
        along = jnp.mean(da * wide, -1, keepdims=True)
        dn = da * scale - wide * (scale * scale * scale * along)
        dh = (dy_buf[slot].astype(F32) + dn.astype(BF16).astype(F32)).astype(BF16)
        a_buf[0, :, at] = dh.T
        for c in range(steps):
            to = pl.ds(c * tile, tile)
            dhid = dot(dh, wd_buf[to, :], NT).astype(BF16).astype(F32)
            dgate_out[slot, c] = (dhid * slope_buf[slot, :, to]).astype(BF16)
            dup_out[slot, c] = (dhid * act_buf[slot, :, to]).astype(BF16)
        start(tile_stores(i, slot))

        ended = tiles - 2 * steps

        @pl.when((i >= ended - steps) & (i < ended))
        def _():
            pass_on(0, i - ended + 2 * steps)

        @pl.when(i >= ended)
        def _():
            finish(0, i - ended, gd1, ggu1)

        return 0

    lax.fori_loop(0, tiles, tile_back, 0)
    for peer in (right, left):
        pl.semaphore_signal(ready, inc=1, device_id={axis: peer}, device_id_type=mesh_id)
    for i in (tiles - 2, tiles - 1):
        for one in tile_stores(i, i % 2):
            one.wait()
    drain(1, steps)
    drain(0, 2 * steps)

    gradients(hid0, dgate0, dup0, None, lambda: pl.semaphore_wait(ready, 2), gd0, ggu0)

    def rest(i, _):
        pass_on(0, steps + i)
        finish(0, i, gd0, ggu0)
        return 0

    def final(i, _):
        finish(0, steps + i, gd0, ggu0)
        return 0

    lax.fori_loop(0, steps, rest, 0)
    lax.fori_loop(0, steps, final, 0)

    norms[3] = total_ref[...]
    copies = [
        pltpu.make_async_remote_copy(
            src_ref=norms.at[3],
            dst_ref=norms.at[to],
            send_sem=norm_sem.at[0, to],
            recv_sem=norm_sem.at[1, to],
            device_id={axis: peer},
            device_id_type=mesh_id,
        )
        for to, peer in enumerate((right, left, across))
    ]
    start(copies)
    drain(1, steps)
    drain(0, 2 * steps)
    for one in copies:
        one.wait()
    total = jnp.sum((norms[0] + norms[1]) + (norms[2] + norms[3]), keepdims=True)
    factor = jnp.minimum(1.0, 0.5 * lax.rsqrt(total / (3.0 * wg.shape[0] * wg.shape[1] * wg.shape[2]) + 1e-30))
    total_ref[...] = jnp.broadcast_to(factor, total_ref.shape)


def back(dy, dy_t, a1, hid1, dgate1, dup1, h1, act0, slope0, hid0, a0, wg, wu, wd, rows_tile=256):
    t, d = dy.shape
    steps, _, tile = hid1.shape
    f = steps * tile
    shapes, counts = ((d // (2 * N), tile), (tile // (2 * N), d)), (2 * steps, steps)

    def each(*parts):
        return [pltpu.VMEM((counts[k], *parts, *shapes[k]), BF16) for k in range(2)]

    any_spec, vmem_spec = pl.BlockSpec(memory_space=pl.ANY), pl.BlockSpec(memory_space=pltpu.VMEM)
    down, gate_up = jax.ShapeDtypeStruct((f // N, d), BF16), jax.ShapeDtypeStruct((2, d // N, f), BF16)
    return pl.pallas_call(
        functools.partial(back_kernel, "dp", tile, rows_tile),
        in_specs=[any_spec] * 14,
        out_specs=[vmem_spec] * 5 + [any_spec] * 2,
        out_shape=[down, down, gate_up, gate_up, jax.ShapeDtypeStruct((8, 128), F32)] + [blocks_shape(t, f)] * 2,
        scratch_shapes=[
            pltpu.VMEM((2, d, t), BF16),
            pltpu.VMEM((2, t, tile), BF16),
            pltpu.VMEM((d, f), BF16),
            pltpu.VMEM((d, f), BF16),
            pltpu.VMEM((f, d), BF16),
            pltpu.VMEM((2, steps, rows_tile, tile), BF16),
            pltpu.VMEM((2, steps, rows_tile, tile), BF16),
            pltpu.VMEM((2, rows_tile, f), F32),
            pltpu.VMEM((2, rows_tile, f), F32),
            pltpu.VMEM((2, rows_tile, d), BF16),
            pltpu.VMEM((2, rows_tile, d), BF16),
            pltpu.VMEM((2, steps, rows_tile, tile), BF16),
            pltpu.VMEM((2, steps, rows_tile, tile), BF16),
            each(2 * N),
            each(2),
            each(2),
            each(),
            each(),
            [pltpu.VMEM((d, tile), BF16), pltpu.VMEM((tile, d), BF16)],
            pltpu.VMEM((4, 8, 128), F32),
            pltpu.SemaphoreType.DMA((2,)),
            pltpu.SemaphoreType.DMA((2,)),
            pltpu.SemaphoreType.DMA((3,)),
            pltpu.SemaphoreType.DMA((2, 6)),
            pltpu.SemaphoreType.DMA((2, 2)),
            pltpu.SemaphoreType.REGULAR,
            pltpu.SemaphoreType.DMA((2, 3)),
            pltpu.SemaphoreType.DMA((4, 3 * steps)),
            pltpu.SemaphoreType.DMA((4, 3 * steps)),
        ],
        compiler_params=pltpu.CompilerParams(vmem_limit_bytes=67_000_000, collective_id=1, has_side_effects=True),
        cost_estimate=cost(18 * t * d * f, 40 * t * f),
        name="back",
    )(dy, dy_t, a1, hid1, dgate1, dup1, h1, act0, slope0, hid0, a0, wg, wu, wd)[:5]


def adamw(w, m, v, g):
    m = 0.9 * m + 0.1 * g
    v = 0.95 * v + 0.05 * g * g
    step = m * lax.rsqrt(v + 1e-8) + 0.1 * w
    return (w - 0.02 * step).astype(BF16), m, v


def update_kernel(me_ref, factor_ref, g_ref, m_ref, v_ref, w_ref, *refs):
    new_w, new_m, new_v = refs[-3:]
    g = g_ref[...].astype(F32) * factor_ref[0:1, 0:1]
    new_w[...], new_m[...], new_v[...] = adamw(w_ref[...].astype(F32), m_ref[...], v_ref[...], g)


def update(me, factor, g, which, m, v, w, layer, into, blocks=2):
    rows, columns = m.shape[1:]
    size = rows // blocks
    own = pl.BlockSpec((None, size, columns), lambda i, me: (layer, i, 0))
    if g.ndim == 3:
        g_spec = pl.BlockSpec((None, size, columns), lambda i, me: (which, i, 0))
    else:
        g_spec = pl.BlockSpec((size, columns), lambda i, me: (i, 0))
    return pl.pallas_call(
        update_kernel,
        grid_spec=pltpu.PrefetchScalarGridSpec(
            num_scalar_prefetch=1,
            grid=(blocks,),
            in_specs=[
                pl.BlockSpec((8, 128), lambda i, me: (0, 0)),
                g_spec,
                own,
                own,
                pl.BlockSpec((None, size, columns), lambda i, me: (layer, me[0] * blocks + i, 0)),
            ]
            + [pl.BlockSpec(memory_space=pl.ANY)] * len(into),
            out_specs=[pl.BlockSpec((size, columns), lambda i, me: (i, 0)), own, own],
        ),
        out_shape=[jax.ShapeDtypeStruct((rows, columns), BF16)] + [jax.ShapeDtypeStruct(m.shape, F32)] * 2,
        input_output_aliases={6 + k: 1 + k for k in range(len(into))},
        compiler_params=params(),
        cost_estimate=cost(2_000_000_000, 22 * rows * columns),
    )(me, factor, g, m, v, w, *into)


def place_kernel(axis, where, *refs):
    blocks, refs = refs[: len(where)], refs[len(where) :]
    outs, sems = refs[-4:-1], refs[-1]
    me = lax.axis_index(axis)
    copies = []
    for k, (matrix, layer, shift, start) in enumerate(where):
        rows = outs[matrix].shape[1] // 4
        at = ((me + shift) % 4) * rows + start
        size = blocks[k].shape[0]
        copies.append(pltpu.make_async_copy(blocks[k], outs[matrix].at[layer, pl.ds(pl.multiple_of(at, 16), size), :], sems.at[k]))
    for one in copies:
        one.start()
    for one in copies:
        one.wait()


def place(blocks, where, shapes, into):
    any_spec, vmem_spec = pl.BlockSpec(memory_space=pl.ANY), pl.BlockSpec(memory_space=pltpu.VMEM)
    into = list(into)
    return pl.pallas_call(
        functools.partial(place_kernel, "dp", where),
        in_specs=[vmem_spec] * len(blocks) + [any_spec] * len(into),
        out_specs=[any_spec] * 3,
        out_shape=[jax.ShapeDtypeStruct(s, BF16) for s in shapes],
        scratch_shapes=[pltpu.SemaphoreType.DMA((len(blocks),))],
        input_output_aliases={len(blocks) + k: k for k in range(len(into))},
        compiler_params=params(),
        cost_estimate=cost(1000, sum(b.size for b in blocks) * 4),
    )(*blocks, *into)


def solution(mesh):
    n = mesh.shape["dp"]
    to_right = [(i, (i + 1) % n) for i in range(n)]
    to_left = [(i, (i - 1) % n) for i in range(n)]

    def body(x, dy, wg, wu, wd, *moments):
        m, v = moments[:3], moments[3:]
        x, dy = x[0], dy[0]
        act0, slope0, hid0, h1, a0, hid1, dgate1, dup1, a1, dy_t = front(x, dy, wg, wu, wd)
        gd0, gd1, ggu0, ggu1, factor = back(dy, dy_t, a1, hid1, dgate1, dup1, h1, act0, slope0, hid0, a0, wg, wu, wd)
        me = lax.axis_index("dp").astype(jnp.int32).reshape(1)
        weights = (wg, wu, wd)
        new, blocks, where, direct = [(), (), ()], [], [], {}
        for k in range(3):
            for layer, g in enumerate((gd0, gd1) if k == 2 else (ggu0, ggu1)):
                own, *new[k] = update(me, factor, g, k, m[k], v[k], weights[k], layer, new[k])
                from_left = lax.ppermute(own, "dp", to_right)
                from_right = lax.ppermute(own, "dp", to_left)
                direct[k, layer] = (from_left, from_right)
                blocks += [own, from_left, from_right]
                where += [(k, layer, 0, 0), (k, layer, n - 1, 0), (k, layer, 1, 0)]
        shapes = [w.shape for w in weights]
        whole = place(blocks, where, shapes, ())
        far = []
        for (k, layer), (from_left, from_right) in direct.items():
            half = from_left.shape[0] // 2
            far += [
                (lax.ppermute(from_left[:half], "dp", to_right), (k, layer, 2, 0)),
                (lax.ppermute(from_right[half:], "dp", to_left), (k, layer, 2, half)),
            ]
        for part in (far[:8], far[8:]):
            whole = place([one[0] for one in part], [one[1] for one in part], shapes, whole)
        return (*whole, *(one[0] for one in new), *(one[1] for one in new))

    whole, rows = P(None, None, None), P(None, "dp", None)
    return jax.shard_map(
        body,
        mesh=mesh,
        in_specs=(P(("rep", "dp")),) * 2 + (whole,) * 3 + (rows,) * 6,
        out_specs=(P("rep"),) * 3 + (P("rep", "dp"),) * 6,
        check_vma=False,
    )
```

profile of v0, /device:TPU:112, one launch (start us, length us, event | category | flops | bytes accessed | tf_op | source)
XLA Modules:
  0.0 425.7 jit_solution(14289828840878869669)
XLA Ops:
  0.6 104.0 %front.1 = (f32[4096,2048]{1,0:T(8,128)}, f32[4096,2048]{1,0:T(8,128)}, bf16[4,4096,512]{2,1,0:T(8,128)(2,1)}, bf16[4096,640]{1,0:T(8,128)(2,1)}, bf16[640,4096]...) custom-call(bf16[4096,640]{1,0:T(8,128)(2,1)} %bitcast.3, ...), custom_call_target="tpu_custom_call" | custom-call | flops 64424509440 | bytes 134217728 | tf_op jit(solution)/shard_map/front/pallas_call | solution.py:104
  104.7 177.3 %back.1 = (bf16[512,640]{1,0:T(8,128)(2,1)}, bf16[512,640]{1,0:T(8,128)(2,1)}, bf16[2,160,2048]{2,1,0:T(8,128)(2,1)}, bf16[2,160,2048]{2,1,0:T(8,128)(2,1)}, f32...) custom-call(bf16[4096,640]{1,0:T(8,128)(2,1)} %bitcast.5, ...), custom_call_target="tpu_custom_call" | custom-call | flops 96636764160 | bytes 335544320 | tf_op jit(solution)/shard_map/back/pallas_call | solution.py:402
  282.0 3.9 shard_map.182
  285.9 3.7 shard_map.183
  290.6 2.4 collective-permute-start.22
  292.9 3.2 collective-permute-start.18
  296.2 3.8 shard_map.180
  300.0 3.8 shard_map.181
  303.9 4.9 %collective-permute-done.20.refs_10_ = bf16[160,2048]{1,0:T(8,128)(2,1)S(1)} collective-permute-done((bf16[160,2048]{1,0:T(8,128)(2,1)}, bf16[160,2048]{1,0:T(8,128)(2,1)S(1)}, u32[]{:S(2)}, u32[]{:S(2)}) %collective-permute-start.20) | collective-permute-done | bytes 655392 | tf_op jit(solution)/shard_map/ppermute | solution.py:534
  309.0 3.1 collective-permute-start.10
  312.1 3.9 shard_map.178
  315.9 3.9 shard_map.179
  319.8 3.1 collective-permute-done.16.refs_7_
  323.1 13.9 %collective-permute-done.12.refs_4_ = bf16[160,2048]{1,0:T(8,128)(2,1)} collective-permute-done((bf16[160,2048]{1,0:T(8,128)(2,1)}, bf16[160,2048]{1,0:T(8,128)(2,1)}, u32[]{:S(2)}, u32[]{:S(2)}) %collective-permute-start.12) | collective-permute-done | bytes 655392 | tf_op jit(solution)/shard_map/ppermute | solution.py:534
  337.2 1.8 collective-permute-start
  338.9 11.7 %collective-permute-done.10.refs_2_ = bf16[160,2048]{1,0:T(8,128)(2,1)} collective-permute-done((bf16[160,2048]{1,0:T(8,128)(2,1)}, bf16[160,2048]{1,0:T(8,128)(2,1)}, u32[]{:S(2)}, u32[]{:S(2)}) %collective-permute-start.10) | collective-permute-done | bytes 655392 | tf_op jit(solution)/shard_map/ppermute | solution.py:535
  350.6 3.6 collective-permute-start.2
  354.2 1.0 slice.59
  355.3 9.5 %collective-permute-done.4.refs_16_ = bf16[512,640]{1,0:T(8,128)(2,1)S(1)} collective-permute-done((bf16[512,640]{1,0:T(8,128)(2,1)}, bf16[512,640]{1,0:T(8,128)(2,1)S(1)}, u32[]{:S(2)}, u32[]{:S(2)}) %collective-permute-start.4) | collective-permute-done | bytes 655392 | tf_op jit(solution)/shard_map/ppermute | solution.py:534
  370.2 1.9 collective-permute-start.17
  372.0 6.9 %collective-permute-done.refs_13_ = bf16[512,640]{1,0:T(8,128)(2,1)S(1)} collective-permute-done((bf16[512,640]{1,0:T(8,128)(2,1)}, bf16[512,640]{1,0:T(8,128)(2,1)S(1)}, u32[]{:S(2)}, u32[]{:S(2)}) %collective-permute-start) | collective-permute-done | bytes 655392 | tf_op jit(solution)/shard_map/ppermute | solution.py:534
  379.2 1.8 collective-permute-start.13
  381.0 5.0 %collective-permute-done.21.refs_6_ = bf16[80,2048]{1,0:T(8,128)(2,1)S(1)} collective-permute-done((bf16[80,2048]{1,0:T(8,128)(2,1)S(1)}, bf16[80,2048]{1,0:T(8,128)(2,1)S(1)}, u32[]{:S(2)}, u32[]{:S(2)}) %collective-permute-start.21) | collective-permute-done | bytes 327712 | tf_op jit(solution)/shard_map/ppermute | solution.py:545
  386.2 3.0 collective-permute-start.11
  390.9 2.1 collective-permute-done.17.refs_4_
  393.2 6.8 %collective-permute-done.13.refs_2_ = bf16[80,2048]{1,0:T(8,128)(2,1)S(1)} collective-permute-done((bf16[80,2048]{1,0:T(8,128)(2,1)S(1)}, bf16[80,2048]{1,0:T(8,128)(2,1)S(1)}, u32[]{:S(2)}, u32[]{:S(2)}) %collective-permute-start.13) | collective-permute-done | bytes 327712 | tf_op jit(solution)/shard_map/ppermute | solution.py:545
  400.3 1.8 collective-permute-start.1
  402.0 4.7 %collective-permute-done.11.refs_1_ = bf16[80,2048]{1,0:T(8,128)(2,1)S(1)} collective-permute-done((bf16[80,2048]{1,0:T(8,128)(2,1)S(1)}, bf16[80,2048]{1,0:T(8,128)(2,1)S(1)}, u32[]{:S(2)}, u32[]{:S(2)}) %collective-permute-start.11) | collective-permute-done | bytes 327712 | tf_op jit(solution)/shard_map/ppermute | solution.py:546
  407.4 3.6 collective-permute-start.3
  411.0 8.8 %shard_map.184 = (bf16[2,640,2048]{2,1,0:T(8,128)(2,1)}, bf16[2,640,2048]{2,1,0:T(8,128)(2,1)}, bf16[2,2048,640]{2,1,0:T(8,128)(2,1)}) custom-call(bf16[160,2048]{1,0:T(8,128)(2,1)} %get-tuple-element.69.refs_0_, bf16[160,2048]{1,0:T(8,128)(2,1)} %copy-done.1, bf16[160,2048]{1,0:T(8,128)(2,1)} %collective-permute-done.10.refs_2_, ...), custom_call_target="tpu_custom_call" | custom-call | flops 1000 | bytes 23592960 | tf_op jit(solution)/shard_map/pallas_call | solution.py:506
  419.9 3.2 shard_map.185
  423.1 2.4 shard_map.186
  (65 shorter events, 10.3 us)
Async XLA Ops:
  289.7 19.0 %collective-permute-start.20 = (bf16[160,2048]{1,0:T(8,128)(2,1)}, bf16[160,2048]{1,0:T(8,128)(2,1)S(1)}, u32[]{:S(2)}, u32[]{:S(2)}) collective-permute-start(bf16[160,2048]{1,0:T(8,128)(2,1)} %get-tuple-element.77.refs_9_), channel_id=1, source_target_pairs={{0,1},{1,2},{2,3},{3,0},{4,5},{5,6},{6,7},{7,4},{8,9},{9,10},{10,1... | collective-permute-start | bytes 1966088 | tf_op jit(solution)/shard_map/ppermute | solution.py:534
  290.6 18.4 %collective-permute-start.22 = (bf16[160,2048]{1,0:T(8,128)(2,1)}, bf16[160,2048]{1,0:T(8,128)(2,1)}, u32[]{:S(2)}, u32[]{:S(2)}) collective-permute-start(bf16[160,2048]{1,0:T(8,128)(2,1)} %get-tuple-element.77.refs_9_), channel_id=1, source_target_pairs={{0,3},{1,0},{2,1},{3,2},{4,7},{5,4},{6,5},{7,6},{8,11},{9,8},{10,9... | collective-permute-start | bytes 1966088 | tf_op jit(solution)/shard_map/ppermute | solution.py:535
  292.9 29.9 %collective-permute-start.16 = (bf16[160,2048]{1,0:T(8,128)(2,1)}, bf16[160,2048]{1,0:T(8,128)(2,1)}, u32[]{:S(2)}, u32[]{:S(2)}) collective-permute-start(bf16[160,2048]{1,0:T(8,128)(2,1)} %get-tuple-element.74.refs_6_), channel_id=1, source_target_pairs={{0,1},{1,2},{2,3},{3,0},{4,5},{5,6},{6,7},{7,4},{8,9},{9,10},{10,1... | collective-permute-start | bytes 1966088 | tf_op jit(solution)/shard_map/ppermute | solution.py:534
  292.9 29.9 %collective-permute-start.18 = (bf16[160,2048]{1,0:T(8,128)(2,1)}, bf16[160,2048]{1,0:T(8,128)(2,1)}, u32[]{:S(2)}, u32[]{:S(2)}) collective-permute-start(bf16[160,2048]{1,0:T(8,128)(2,1)} %get-tuple-element.74.refs_6_), channel_id=1, source_target_pairs={{0,3},{1,0},{2,1},{3,2},{4,7},{5,4},{6,5},{7,6},{8,11},{9,8},{10,9... | collective-permute-start | bytes 1966088 | tf_op jit(solution)/shard_map/ppermute | solution.py:535
  303.8 33.1 %collective-permute-start.12 = (bf16[160,2048]{1,0:T(8,128)(2,1)}, bf16[160,2048]{1,0:T(8,128)(2,1)}, u32[]{:S(2)}, u32[]{:S(2)}) collective-permute-start(bf16[160,2048]{1,0:T(8,128)(2,1)} %get-tuple-element.73.refs_3_), channel_id=1, source_target_pairs={{0,1},{1,2},{2,3},{3,0},{4,5},{5,6},{6,7},{7,4},{8,9},{9,10},{10,1... | collective-permute-start | bytes 1966088 | tf_op jit(solution)/shard_map/ppermute | solution.py:534
  308.7 45.5 %copy-start = (bf16[160,2048]{1,0:T(8,128)(2,1)}, bf16[160,2048]{1,0:T(8,128)(2,1)S(1)}, u32[]{:S(2)}) copy-start(bf16[160,2048]{1,0:T(8,128)(2,1)S(1)} %collective-permute-done.20.refs_10_) | copy-start | bytes 1966084
  308.7 28.4 %collective-permute-start.14 = (bf16[160,2048]{1,0:T(8,128)(2,1)}, bf16[160,2048]{1,0:T(8,128)(2,1)}, u32[]{:S(2)}, u32[]{:S(2)}) collective-permute-start(bf16[160,2048]{1,0:T(8,128)(2,1)} %get-tuple-element.73.refs_3_), channel_id=1, source_target_pairs={{0,3},{1,0},{2,1},{3,2},{4,7},{5,4},{6,5},{7,6},{8,11},{9,8},{10,9... | collective-permute-start | bytes 1966088 | tf_op jit(solution)/shard_map/ppermute | solution.py:535
  309.0 41.6 %collective-permute-start.10 = (bf16[160,2048]{1,0:T(8,128)(2,1)}, bf16[160,2048]{1,0:T(8,128)(2,1)}, u32[]{:S(2)}, u32[]{:S(2)}) collective-permute-start(bf16[160,2048]{1,0:T(8,128)(2,1)} %get-tuple-element.69.refs_0_), channel_id=1, source_target_pairs={{0,3},{1,0},{2,1},{3,2},{4,7},{5,4},{6,5},{7,6},{8,11},{9,8},{10,9... | collective-permute-start | bytes 1966088 | tf_op jit(solution)/shard_map/ppermute | solution.py:535
  322.9 32.4 %collective-permute-start.8 = (bf16[160,2048]{1,0:T(8,128)(2,1)}, bf16[160,2048]{1,0:T(8,128)(2,1)S(1)}, u32[]{:S(2)}, u32[]{:S(2)}) collective-permute-start(bf16[160,2048]{1,0:T(8,128)(2,1)} %get-tuple-element.69.refs_0_), channel_id=1, source_target_pairs={{0,1},{1,2},{2,3},{3,0},{4,5},{5,6},{6,7},{7,4},{8,9},{9,10},{10,1... | collective-permute-start | bytes 1966088 | tf_op jit(solution)/shard_map/ppermute | solution.py:534
  322.9 42.0 %collective-permute-start.4 = (bf16[512,640]{1,0:T(8,128)(2,1)}, bf16[512,640]{1,0:T(8,128)(2,1)S(1)}, u32[]{:S(2)}, u32[]{:S(2)}) collective-permute-start(bf16[512,640]{1,0:T(8,128)(2,1)} %get-tuple-element.67.refs_15_), channel_id=1, source_target_pairs={{0,1},{1,2},{2,3},{3,0},{4,5},{5,6},{6,7},{7,4},{8,9},{9,10},{10,1... | collective-permute-start | bytes 1966088 | tf_op jit(solution)/shard_map/ppermute | solution.py:534
  336.9 33.2 %collective-permute-start.6 = (bf16[512,640]{1,0:T(8,128)(2,1)}, bf16[512,640]{1,0:T(8,128)(2,1)S(1)}, u32[]{:S(2)}, u32[]{:S(2)}) collective-permute-start(bf16[512,640]{1,0:T(8,128)(2,1)} %get-tuple-element.67.refs_15_), channel_id=1, source_target_pairs={{0,3},{1,0},{2,1},{3,2},{4,7},{5,4},{6,5},{7,6},{8,11},{9,8},{10,9... | collective-permute-start | bytes 1966088 | tf_op jit(solution)/shard_map/ppermute | solution.py:535
  337.2 41.8 %collective-permute-start = (bf16[512,640]{1,0:T(8,128)(2,1)}, bf16[512,640]{1,0:T(8,128)(2,1)S(1)}, u32[]{:S(2)}, u32[]{:S(2)}) collective-permute-start(bf16[512,640]{1,0:T(8,128)(2,1)} %get-tuple-element.63.refs_12_), channel_id=1, source_target_pairs={{0,1},{1,2},{2,3},{3,0},{4,5},{5,6},{6,7},{7,4},{8,9},{9,10},{10,1... | collective-permute-start | bytes 1966088 | tf_op jit(solution)/shard_map/ppermute | solution.py:534
  350.6 28.6 %collective-permute-start.2 = (bf16[512,640]{1,0:T(8,128)(2,1)}, bf16[512,640]{1,0:T(8,128)(2,1)S(1)}, u32[]{:S(2)}, u32[]{:S(2)}) collective-permute-start(bf16[512,640]{1,0:T(8,128)(2,1)} %get-tuple-element.63.refs_12_), channel_id=1, source_target_pairs={{0,3},{1,0},{2,1},{3,2},{4,7},{5,4},{6,5},{7,6},{8,11},{9,8},{10,9... | collective-permute-start | bytes 1966088 | tf_op jit(solution)/shard_map/ppermute | solution.py:535
  355.2 34.0 %copy-start.1 = (bf16[160,2048]{1,0:T(8,128)(2,1)}, bf16[160,2048]{1,0:T(8,128)(2,1)S(1)}, u32[]{:S(2)}) copy-start(bf16[160,2048]{1,0:T(8,128)(2,1)S(1)} %collective-permute-done.8.refs_1_) | copy-start | bytes 1966084
  355.2 30.7 %collective-permute-start.21 = (bf16[80,2048]{1,0:T(8,128)(2,1)S(1)}, bf16[80,2048]{1,0:T(8,128)(2,1)S(1)}, u32[]{:S(2)}, u32[]{:S(2)}) collective-permute-start(bf16[80,2048]{1,0:T(8,128)(2,1)S(1)} %slice.58), channel_id=1, source_target_pairs={{0,1},{1,2},{2,3},{3,0},{4,5},{5,6},{6,7},{7,4},{8,9},{9,10},{10,1... | collective-permute-start | bytes 983048 | tf_op jit(solution)/shard_map/ppermute | solution.py:545
  364.9 25.1 %copy-start.2 = (bf16[512,640]{1,0:T(8,128)(2,1)}, bf16[512,640]{1,0:T(8,128)(2,1)S(1)}, u32[]{:S(2)}) copy-start(bf16[512,640]{1,0:T(8,128)(2,1)S(1)} %collective-permute-done.4.refs_16_) | copy-start | bytes 1966084
  364.9 21.3 %collective-permute-start.23 = (bf16[80,2048]{1,0:T(8,128)(2,1)S(1)}, bf16[80,2048]{1,0:T(8,128)(2,1)S(1)}, u32[]{:S(2)}, u32[]{:S(2)}) collective-permute-start(bf16[80,2048]{1,0:T(8,128)(2,1)S(1)} %slice.59), channel_id=1, source_target_pairs={{0,3},{1,0},{2,1},{3,2},{4,7},{5,4},{6,5},{7,6},{8,11},{9,8},{10,9... | collective-permute-start | bytes 983048 | tf_op jit(solution)/shard_map/ppermute | solution.py:546
  370.1 20.6 %copy-start.3 = (bf16[512,640]{1,0:T(8,128)(2,1)}, bf16[512,640]{1,0:T(8,128)(2,1)S(1)}, u32[]{:S(2)}) copy-start(bf16[512,640]{1,0:T(8,128)(2,1)S(1)} %collective-permute-done.6.refs_17_) | copy-start | bytes 1966084
  370.2 22.8 %collective-permute-start.17 = (bf16[80,2048]{1,0:T(8,128)(2,1)S(1)}, bf16[80,2048]{1,0:T(8,128)(2,1)S(1)}, u32[]{:S(2)}, u32[]{:S(2)}) collective-permute-start(bf16[80,2048]{1,0:T(8,128)(2,1)S(1)} %slice.56), channel_id=1, source_target_pairs={{0,1},{1,2},{2,3},{3,0},{4,5},{5,6},{6,7},{7,4},{8,9},{9,10},{10,1... | collective-permute-start | bytes 983048 | tf_op jit(solution)/shard_map/ppermute | solution.py:545
  378.9 14.1 %collective-permute-start.19 = (bf16[80,2048]{1,0:T(8,128)(2,1)S(1)}, bf16[80,2048]{1,0:T(8,128)(2,1)S(1)}, u32[]{:S(2)}, u32[]{:S(2)}) collective-permute-start(bf16[80,2048]{1,0:T(8,128)(2,1)S(1)} %slice.57), channel_id=1, source_target_pairs={{0,3},{1,0},{2,1},{3,2},{4,7},{5,4},{6,5},{7,6},{8,11},{9,8},{10,9... | collective-permute-start | bytes 983048 | tf_op jit(solution)/shard_map/ppermute | solution.py:546
  379.2 20.8 %collective-permute-start.13 = (bf16[80,2048]{1,0:T(8,128)(2,1)S(1)}, bf16[80,2048]{1,0:T(8,128)(2,1)S(1)}, u32[]{:S(2)}, u32[]{:S(2)}) collective-permute-start(bf16[80,2048]{1,0:T(8,128)(2,1)S(1)} %slice.54), channel_id=1, source_target_pairs={{0,1},{1,2},{2,3},{3,0},{4,5},{5,6},{6,7},{7,4},{8,9},{9,10},{10,1... | collective-permute-start | bytes 983048 | tf_op jit(solution)/shard_map/ppermute | solution.py:545
  386.0 20.7 %copy-start.6 = (bf16[80,2048]{1,0:T(8,128)(2,1)}, bf16[80,2048]{1,0:T(8,128)(2,1)S(1)}, u32[]{:S(2)}) copy-start(bf16[80,2048]{1,0:T(8,128)(2,1)S(1)} %collective-permute-done.21.refs_6_) | copy-start | bytes 983044
  386.0 14.3 %collective-permute-start.15 = (bf16[80,2048]{1,0:T(8,128)(2,1)S(1)}, bf16[80,2048]{1,0:T(8,128)(2,1)S(1)}, u32[]{:S(2)}, u32[]{:S(2)}) collective-permute-start(bf16[80,2048]{1,0:T(8,128)(2,1)S(1)} %slice.55), channel_id=1, source_target_pairs={{0,3},{1,0},{2,1},{3,2},{4,7},{5,4},{6,5},{7,6},{8,11},{9,8},{10,9... | collective-permute-start | bytes 983048 | tf_op jit(solution)/shard_map/ppermute | solution.py:546
  386.2 20.5 %copy-start.7 = (bf16[80,2048]{1,0:T(8,128)(2,1)}, bf16[80,2048]{1,0:T(8,128)(2,1)S(1)}, u32[]{:S(2)}) copy-start(bf16[80,2048]{1,0:T(8,128)(2,1)S(1)} %collective-permute-done.23.refs_7_) | copy-start | bytes 983044
  386.2 20.5 %collective-permute-start.11 = (bf16[80,2048]{1,0:T(8,128)(2,1)S(1)}, bf16[80,2048]{1,0:T(8,128)(2,1)S(1)}, u32[]{:S(2)}, u32[]{:S(2)}) collective-permute-start(bf16[80,2048]{1,0:T(8,128)(2,1)S(1)} %slice.53), channel_id=1, source_target_pairs={{0,3},{1,0},{2,1},{3,2},{4,7},{5,4},{6,5},{7,6},{8,11},{9,8},{10,9... | collective-permute-start | bytes 983048 | tf_op jit(solution)/shard_map/ppermute | solution.py:546
  393.0 13.7 %copy-start.8 = (bf16[80,2048]{1,0:T(8,128)(2,1)}, bf16[80,2048]{1,0:T(8,128)(2,1)S(1)}, u32[]{:S(2)}) copy-start(bf16[80,2048]{1,0:T(8,128)(2,1)S(1)} %collective-permute-done.17.refs_4_) | copy-start | bytes 983044
  393.0 26.9 %collective-permute-start.9 = (bf16[80,2048]{1,0:T(8,128)(2,1)}, bf16[80,2048]{1,0:T(8,128)(2,1)}, u32[]{:S(2)}, u32[]{:S(2)}) collective-permute-start(bf16[80,2048]{1,0:T(8,128)(2,1)} %slice.52), channel_id=1, source_target_pairs={{0,1},{1,2},{2,3},{3,0},{4,5},{5,6},{6,7},{7,4},{8,9},{9,10},{10,1... | collective-permute-start | bytes 983048 | tf_op jit(solution)/shard_map/ppermute | solution.py:545
  393.0 13.7 %copy-start.9 = (bf16[80,2048]{1,0:T(8,128)(2,1)}, bf16[80,2048]{1,0:T(8,128)(2,1)S(1)}, u32[]{:S(2)}) copy-start(bf16[80,2048]{1,0:T(8,128)(2,1)S(1)} %collective-permute-done.19.refs_5_) | copy-start | bytes 983044
  393.0 30.1 %collective-permute-start.5 = (bf16[256,640]{1,0:T(8,128)(2,1)}, bf16[256,640]{1,0:T(8,128)(2,1)}, u32[]{:S(2)}, u32[]{:S(2)}) collective-permute-start(bf16[256,640]{1,0:T(8,128)(2,1)} %slice.50), channel_id=1, source_target_pairs={{0,1},{1,2},{2,3},{3,0},{4,5},{5,6},{6,7},{7,4},{8,9},{9,10},{10,1... | collective-permute-start | bytes 983048 | tf_op jit(solution)/shard_map/ppermute | solution.py:545
  400.0 23.1 %collective-permute-start.7 = (bf16[256,640]{1,0:T(8,128)(2,1)S(1)}, bf16[256,640]{1,0:T(8,128)(2,1)}, u32[]{:S(2)}, u32[]{:S(2)}) collective-permute-start(bf16[256,640]{1,0:T(8,128)(2,1)S(1)} %slice.51), channel_id=1, source_target_pairs={{0,3},{1,0},{2,1},{3,2},{4,7},{5,4},{6,5},{7,6},{8,11},{9,8},{10,9... | collective-permute-start | bytes 983048 | tf_op jit(solution)/shard_map/ppermute | solution.py:546
  400.3 22.9 %collective-permute-start.1 = (bf16[256,640]{1,0:T(8,128)(2,1)S(1)}, bf16[256,640]{1,0:T(8,128)(2,1)}, u32[]{:S(2)}, u32[]{:S(2)}) collective-permute-start(bf16[256,640]{1,0:T(8,128)(2,1)S(1)} %slice.48), channel_id=1, source_target_pairs={{0,1},{1,2},{2,3},{3,0},{4,5},{5,6},{6,7},{7,4},{8,9},{9,10},{10,1... | collective-permute-start | bytes 983048 | tf_op jit(solution)/shard_map/ppermute | solution.py:545
  407.4 15.7 %collective-permute-start.3 = (bf16[256,640]{1,0:T(8,128)(2,1)S(1)}, bf16[256,640]{1,0:T(8,128)(2,1)}, u32[]{:S(2)}, u32[]{:S(2)}) collective-permute-start(bf16[256,640]{1,0:T(8,128)(2,1)S(1)} %slice.49), channel_id=1, source_target_pairs={{0,3},{1,0},{2,1},{3,2},{4,7},{5,4},{6,5},{7,6},{8,11},{9,8},{10,9... | collective-permute-start | bytes 983048 | tf_op jit(solution)/shard_map/ppermute | solution.py:546
  (5 other events, 37.3 us)
where the time goes:
time: 426 us
  Pallas kernels  319 us (75%)
  waiting for transfers between devices  68.5 us (16%)
  starting transfers between devices  28.8 us (7%)
  local copies, waits for them, and re-layouts  8.37 us (2%)
    pallas_call x1, Pallas kernels, back(): pl.pallas_call(functools.partial(back_kernel, 'dp', tile, rows_tile), in_...  177 us
    pallas_call x1, Pallas kernels, front(): pl.pallas_call(front_kernel, grid=(t // tile,), in_specs=[tokens] * 2 + [...  104 us
    ppermute x6, waiting for transfers between devices, body(): from_left = lax.ppermute(own, 'dp', to_right)  38.2 us
    pallas_call x6, Pallas kernels, update(): pl.pallas_call(update_kernel, grid_spec=pltpu.PrefetchScalarGridSpec(num_...  23 us
    pallas_call x3, Pallas kernels, place(): pl.pallas_call(functools.partial(place_kernel, 'dp', where), in_specs=[vm...  14.4 us
    ppermute x6, waiting for transfers between devices, body(): lax.ppermute(from_left[:half], 'dp', to_right)  13.9 us
    ppermute x6, starting transfers between devices, body(): from_right = lax.ppermute(own, 'dp', to_left)  12.8 us
    ppermute x6, waiting for transfers between devices, body(): from_right = lax.ppermute(own, 'dp', to_left)  11.7 us
  transfers between devices with their start and end apart: 24, of which 10 were waited for; matrix products, arithmetic and copies ran while one was open for 2% of the time, Pallas kernels for 6%

commit v1 on v0

--- a/solution.py
+++ b/solution.py
@@ -232,6 +232,8 @@
             load_b(dgate, i % steps, slot).wait()
             put(0, i, dot(a_buf[1], b_buf[slot]))
 
+            start(sends(0, i, (0, 1)))
+
             @pl.when(i < steps - 2)
             def _():
                 load_b(dgate, i + 2, slot).start()
@@ -245,8 +247,6 @@
                 @pl.when(i >= 2 * steps - 2)
                 def _():
                     load_b(next_hid, i + 2 - 2 * steps, slot).start()
-
-            start(sends(0, i, (0, 1)))
 
             @pl.when(i < steps)
             def _():
@@ -454,9 +454,10 @@
     new_w[...], new_m[...], new_v[...] = adamw(w_ref[...].astype(F32), m_ref[...], v_ref[...], g)
 
 
-def update(me, factor, g, which, m, v, w, layer, into, blocks=2):
+def update(me, factor, g, which, m, v, w, layer, into):
     rows, columns = m.shape[1:]
-    size = rows // blocks
+    size = 32 if rows < 256 else 128
+    blocks = rows // size
     own = pl.BlockSpec((None, size, columns), lambda i, me: (layer, i, 0))
     if g.ndim == 3:
         g_spec = pl.BlockSpec((None, size, columns), lambda i, me: (which, i, 0))
@@ -545,7 +546,7 @@
                 (lax.ppermute(from_left[:half], "dp", to_right), (k, layer, 2, 0)),
                 (lax.ppermute(from_right[half:], "dp", to_left), (k, layer, 2, half)),
             ]
-        for part in (far[:8], far[8:]):
+        for part in (far[:10], far[10:]):
             whole = place([one[0] for one in part], [one[1] for one in part], shapes, whole)
         return (*whole, *(one[0] for one in new), *(one[1] for one in new))
 

time: 426 us -> 427 us (level)
  Pallas kernels: 319 us -> 326 us
  waiting for transfers between devices: 68.5 us -> 64 us
    pallas_call x6, Pallas kernels: 23 us -> 30.6 us  [update(): pl.pallas_call(update_kernel, grid_spec=pltpu.PrefetchScalarGridSpec(num_...]
  transfers between devices with their start and end apart: 24 -> 24, of which waited for: 10 -> 10; matrix products, arithmetic and copies ran while one was open for 2% -> 2% of each run, Pallas kernels for 6% -> 8%
where the time goes in v1:
time: 427 us; the launch traced here: 426 us
  Pallas kernels  326 us (76%)
  waiting for transfers between devices  64 us (15%)
  starting transfers between devices  26.1 us (6%)
  local copies, waits for them, and re-layouts  8.4 us (2%)
    pallas_call x1, Pallas kernels, back(): pl.pallas_call(functools.partial(back_kernel, 'dp', tile, rows_tile), in_...  177 us
    pallas_call x1, Pallas kernels, front(): pl.pallas_call(front_kernel, grid=(t // tile,), in_specs=[tokens] * 2 + [...  104 us
    ppermute x6, waiting for transfers between devices, body(): from_left = lax.ppermute(own, 'dp', to_right)  36.9 us
    pallas_call x6, Pallas kernels, update(): pl.pallas_call(update_kernel, grid_spec=pltpu.PrefetchScalarGridSpec(num_...  30.6 us
    pallas_call x3, Pallas kernels, place(): pl.pallas_call(functools.partial(place_kernel, 'dp', where), in_specs=[vm...  14.4 us
    ppermute x6, waiting for transfers between devices, body(): from_right = lax.ppermute(own, 'dp', to_left)  11.7 us
    ppermute x6, waiting for transfers between devices, body(): lax.ppermute(from_left[:half], 'dp', to_right)  10.6 us
    ppermute x6, starting transfers between devices, body(): from_right = lax.ppermute(own, 'dp', to_left)  9.69 us
  transfers between devices with their start and end apart: 24, of which 10 were waited for; matrix products, arithmetic and copies ran while one was open for 2% of the time, Pallas kernels for 8%

profile of v1, /device:TPU:112, one launch (start us, length us, event | category | flops | bytes accessed | tf_op | source)
XLA Modules:
  0.0 426.0 jit_solution(2646878360434239306)
XLA Ops:
  0.6 104.0 %front.1 = (f32[4096,2048]{1,0:T(8,128)}, f32[4096,2048]{1,0:T(8,128)}, bf16[4,4096,512]{2,1,0:T(8,128)(2,1)}, bf16[4096,640]{1,0:T(8,128)(2,1)}, bf16[640,4096]...) custom-call(bf16[4096,640]{1,0:T(8,128)(2,1)} %bitcast.3, ...), custom_call_target="tpu_custom_call" | custom-call | flops 64424509440 | bytes 134217728 | tf_op jit(solution)/shard_map/front/pallas_call | solution.py:104
  104.7 177.3 %back.1 = (bf16[512,640]{1,0:T(8,128)(2,1)}, bf16[512,640]{1,0:T(8,128)(2,1)}, bf16[2,160,2048]{2,1,0:T(8,128)(2,1)}, bf16[2,160,2048]{2,1,0:T(8,128)(2,1)}, f32...) custom-call(bf16[4096,640]{1,0:T(8,128)(2,1)} %bitcast.5, ...), custom_call_target="tpu_custom_call" | custom-call | flops 96636764160 | bytes 335544320 | tf_op jit(solution)/shard_map/back/pallas_call | solution.py:402
  282.0 5.4 %shard_map.182 = (bf16[160,2048]{1,0:T(8,128)(2,1)}, f32[2,160,2048]{2,1,0:T(8,128)}, f32[2,160,2048]{2,1,0:T(8,128)}) custom-call(s32[1]{0:T(128)} %bitcast.me_ref, f32[8,128]{1,0:T(8,128)} %get-tuple-element.61.factor_ref, bf16[2,160,2048]{2,1,0:T(8,128)(2,1)} %get-tuple-element.67.g_ref, f32[2,160,2048]{2,1,0:T(8,128)} %m_ref.11, f32[2,160,2048]{2,1,0:T(8,128)} %v_ref.11, ...), custom_call_target="tpu_custom_call" | custom-call | flops 2000000000 | bytes 7208960 | tf_op jit(solution)/shard_map/pallas_call | solution.py:466
  287.5 5.4 %shard_map.183 = (bf16[160,2048]{1,0:T(8,128)(2,1)}, f32[2,160,2048]{2,1,0:T(8,128)}, f32[2,160,2048]{2,1,0:T(8,128)}) custom-call(s32[1]{0:T(128)} %bitcast.me_ref, f32[8,128]{1,0:T(8,128)} %get-tuple-element.61.factor_ref, bf16[2,160,2048]{2,1,0:T(8,128)(2,1)} %get-tuple-element.69.g_ref, ...), custom_call_target="tpu_custom_call", output_to_operand_aliasing={{1}: (6, {}), {2}: (7, {})} | custom-call | flops 2000000000 | bytes 7208960 | tf_op jit(solution)/shard_map/pallas_call | solution.py:466
  293.7 2.3 collective-permute-start.18
  296.1 3.2 collective-permute-start.14
  299.3 5.4 %shard_map.180 = (bf16[160,2048]{1,0:T(8,128)(2,1)}, f32[2,160,2048]{2,1,0:T(8,128)}, f32[2,160,2048]{2,1,0:T(8,128)}) custom-call(s32[1]{0:T(128)} %bitcast.me_ref, f32[8,128]{1,0:T(8,128)} %get-tuple-element.61.factor_ref, bf16[2,160,2048]{2,1,0:T(8,128)(2,1)} %get-tuple-element.67.g_ref, f32[2,160,2048]{2,1,0:T(8,128)} %m_ref.9, f32[2,160,2048]{2,1,0:T(8,128)} %v_ref.9, ...), custom_call_target="tpu_custom_call" | custom-call | flops 2000000000 | bytes 7208960 | tf_op jit(solution)/shard_map/pallas_call | solution.py:466
  304.7 5.4 %shard_map.181 = (bf16[160,2048]{1,0:T(8,128)(2,1)}, f32[2,160,2048]{2,1,0:T(8,128)}, f32[2,160,2048]{2,1,0:T(8,128)}) custom-call(s32[1]{0:T(128)} %bitcast.me_ref, f32[8,128]{1,0:T(8,128)} %get-tuple-element.61.factor_ref, bf16[2,160,2048]{2,1,0:T(8,128)(2,1)} %get-tuple-element.69.g_ref, ...), custom_call_target="tpu_custom_call", output_to_operand_aliasing={{1}: (6, {}), {2}: (7, {})} | custom-call | flops 2000000000 | bytes 7208960 | tf_op jit(solution)/shard_map/pallas_call | solution.py:466
  310.1 1.7 collective-permute-done.16.refs_10_
  312.2 4.5 %shard_map.178 = (bf16[512,640]{1,0:T(8,128)(2,1)}, f32[2,512,640]{2,1,0:T(8,128)}, f32[2,512,640]{2,1,0:T(8,128)}) custom-call(s32[1]{0:T(128)} %bitcast.me_ref, f32[8,128]{1,0:T(8,128)} %get-tuple-element.61.factor_ref, bf16[512,640]{1,0:T(8,128)(2,1)} %get-tuple-element.63.g_ref, f32[2,512,640]{2,1,0:T(8,128)} %m_ref.7, f32[2,512,640]{2,1,0:T(8,128)} %v_ref.7, ...), custom_call_target="tpu_custom_call" | custom-call | flops 2000000000 | bytes 7208960 | tf_op jit(solution)/shard_map/pallas_call | solution.py:466
  316.8 4.5 %shard_map.179 = (bf16[512,640]{1,0:T(8,128)(2,1)}, f32[2,512,640]{2,1,0:T(8,128)}, f32[2,512,640]{2,1,0:T(8,128)}) custom-call(s32[1]{0:T(128)} %bitcast.me_ref, f32[8,128]{1,0:T(8,128)} %get-tuple-element.61.factor_ref, bf16[512,640]{1,0:T(8,128)(2,1)} %get-tuple-element.62.g_ref, ...), custom_call_target="tpu_custom_call", output_to_operand_aliasing={{1}: (6, {}), {2}: (7, {})} | custom-call | flops 2000000000 | bytes 7208960 | tf_op jit(solution)/shard_map/pallas_call | solution.py:466
  321.3 4.7 %collective-permute-done.12.refs_7_ = bf16[160,2048]{1,0:T(8,128)(2,1)} collective-permute-done((bf16[160,2048]{1,0:T(8,128)(2,1)}, bf16[160,2048]{1,0:T(8,128)(2,1)}, u32[]{:S(2)}, u32[]{:S(2)}) %collective-permute-start.12) | collective-permute-done | bytes 655392 | tf_op jit(solution)/shard_map/ppermute | solution.py:535
  326.3 1.7 collective-permute-start
  328.0 11.7 %collective-permute-done.10.refs_5_ = bf16[160,2048]{1,0:T(8,128)(2,1)} collective-permute-done((bf16[160,2048]{1,0:T(8,128)(2,1)}, bf16[160,2048]{1,0:T(8,128)(2,1)}, u32[]{:S(2)}, u32[]{:S(2)}) %collective-permute-start.10) | collective-permute-done | bytes 655392 | tf_op jit(solution)/shard_map/ppermute | solution.py:536
  339.8 3.5 collective-permute-start.2
  343.3 10.8 %collective-permute-done.4.refs_1_ = bf16[160,2048]{1,0:T(8,128)(2,1)} collective-permute-done((bf16[160,2048]{1,0:T(8,128)(2,1)}, bf16[160,2048]{1,0:T(8,128)(2,1)}, u32[]{:S(2)}, u32[]{:S(2)}) %collective-permute-start.4) | collective-permute-done | bytes 655392 | tf_op jit(solution)/shard_map/ppermute | solution.py:535
  354.4 1.0 slice.57
  355.4 1.8 collective-permute-start.17
  357.2 10.8 %collective-permute-done.refs_16_ = bf16[512,640]{1,0:T(8,128)(2,1)S(1)} collective-permute-done((bf16[512,640]{1,0:T(8,128)(2,1)}, bf16[512,640]{1,0:T(8,128)(2,1)S(1)}, u32[]{:S(2)}, u32[]{:S(2)}) %collective-permute-start) | collective-permute-done | bytes 655392 | tf_op jit(solution)/shard_map/ppermute | solution.py:535
  369.3 1.0 slice.55
  371.3 1.8 collective-permute-start.13
  373.2 8.9 %collective-permute-done.20.refs_13_ = bf16[512,640]{1,0:T(8,128)(2,1)S(1)} collective-permute-done((bf16[512,640]{1,0:T(8,128)(2,1)}, bf16[512,640]{1,0:T(8,128)(2,1)S(1)}, u32[]{:S(2)}, u32[]{:S(2)}) %collective-permute-start.20) | collective-permute-done | bytes 655392 | tf_op jit(solution)/shard_map/ppermute | solution.py:535
  382.4 2.9 collective-permute-start.11
  387.3 1.8 collective-permute-done.17.refs_6_
  390.2 5.9 %collective-permute-done.13.refs_4_ = bf16[80,2048]{1,0:T(8,128)(2,1)S(1)} collective-permute-done((bf16[80,2048]{1,0:T(8,128)(2,1)S(1)}, bf16[80,2048]{1,0:T(8,128)(2,1)S(1)}, u32[]{:S(2)}, u32[]{:S(2)}) %collective-permute-start.13) | collective-permute-done | bytes 327712 | tf_op jit(solution)/shard_map/ppermute | solution.py:546
  396.4 1.7 collective-permute-start.21
  398.2 4.7 %collective-permute-done.11.refs_3_ = bf16[80,2048]{1,0:T(8,128)(2,1)S(1)} collective-permute-done((bf16[80,2048]{1,0:T(8,128)(2,1)S(1)}, bf16[80,2048]{1,0:T(8,128)(2,1)S(1)}, u32[]{:S(2)}, u32[]{:S(2)}) %collective-permute-start.11) | collective-permute-done | bytes 327712 | tf_op jit(solution)/shard_map/ppermute | solution.py:547
  402.8 3.5 collective-permute-start.23
  407.3 2.8 collective-permute-done.5.refs_0_
  411.3 8.8 %shard_map.184 = (bf16[2,640,2048]{2,1,0:T(8,128)(2,1)}, bf16[2,640,2048]{2,1,0:T(8,128)(2,1)}, bf16[2,2048,640]{2,1,0:T(8,128)(2,1)}) custom-call(bf16[160,2048]{1,0:T(8,128)(2,1)} %get-tuple-element.68.refs_0_, bf16[160,2048]{1,0:T(8,128)(2,1)} %collective-permute-done.4.refs_1_, bf16[160,2048]{1,0:T(8,128)(2,1)} %copy-done.1, ...), custom_call_target="tpu_custom_call" | custom-call | flops 1000 | bytes 23592960 | tf_op jit(solution)/shard_map/pallas_call | solution.py:507
  420.2 3.7 shard_map.185
  423.9 1.9 shard_map.186
  (65 shorter events, 9.9 us)
Async XLA Ops:
  292.8 19.0 %collective-permute-start.16 = (bf16[160,2048]{1,0:T(8,128)(2,1)}, bf16[160,2048]{1,0:T(8,128)(2,1)S(1)}, u32[]{:S(2)}, u32[]{:S(2)}) collective-permute-start(bf16[160,2048]{1,0:T(8,128)(2,1)} %get-tuple-element.76.refs_9_), channel_id=1, source_target_pairs={{0,1},{1,2},{2,3},{3,0},{4,5},{5,6},{6,7},{7,4},{8,9},{9,10},{10,1... | collective-permute-start | bytes 1966088 | tf_op jit(solution)/shard_map/ppermute | solution.py:535
  293.7 18.4 %collective-permute-start.18 = (bf16[160,2048]{1,0:T(8,128)(2,1)}, bf16[160,2048]{1,0:T(8,128)(2,1)}, u32[]{:S(2)}, u32[]{:S(2)}) collective-permute-start(bf16[160,2048]{1,0:T(8,128)(2,1)} %get-tuple-element.76.refs_9_), channel_id=1, source_target_pairs={{0,3},{1,0},{2,1},{3,2},{4,7},{5,4},{6,5},{7,6},{8,11},{9,8},{10,9... | collective-permute-start | bytes 1966088 | tf_op jit(solution)/shard_map/ppermute | solution.py:536
  296.1 29.9 %collective-permute-start.12 = (bf16[160,2048]{1,0:T(8,128)(2,1)}, bf16[160,2048]{1,0:T(8,128)(2,1)}, u32[]{:S(2)}, u32[]{:S(2)}) collective-permute-start(bf16[160,2048]{1,0:T(8,128)(2,1)} %get-tuple-element.73.refs_6_), channel_id=1, source_target_pairs={{0,1},{1,2},{2,3},{3,0},{4,5},{5,6},{6,7},{7,4},{8,9},{9,10},{10,1... | collective-permute-start | bytes 1966088 | tf_op jit(solution)/shard_map/ppermute | solution.py:535
  296.1 30.2 %collective-permute-start.14 = (bf16[160,2048]{1,0:T(8,128)(2,1)}, bf16[160,2048]{1,0:T(8,128)(2,1)}, u32[]{:S(2)}, u32[]{:S(2)}) collective-permute-start(bf16[160,2048]{1,0:T(8,128)(2,1)} %get-tuple-element.73.refs_6_), channel_id=1, source_target_pairs={{0,3},{1,0},{2,1},{3,2},{4,7},{5,4},{6,5},{7,6},{8,11},{9,8},{10,9... | collective-permute-start | bytes 1966088 | tf_op jit(solution)/shard_map/ppermute | solution.py:536
  310.1 29.7 %collective-permute-start.10 = (bf16[160,2048]{1,0:T(8,128)(2,1)}, bf16[160,2048]{1,0:T(8,128)(2,1)}, u32[]{:S(2)}, u32[]{:S(2)}) collective-permute-start(bf16[160,2048]{1,0:T(8,128)(2,1)} %get-tuple-element.72.refs_3_), channel_id=1, source_target_pairs={{0,3},{1,0},{2,1},{3,2},{4,7},{5,4},{6,5},{7,6},{8,11},{9,8},{10,9... | collective-permute-start | bytes 1966088 | tf_op jit(solution)/shard_map/ppermute | solution.py:536
  311.9 42.5 %copy-start = (bf16[160,2048]{1,0:T(8,128)(2,1)}, bf16[160,2048]{1,0:T(8,128)(2,1)S(1)}, u32[]{:S(2)}) copy-start(bf16[160,2048]{1,0:T(8,128)(2,1)S(1)} %collective-permute-done.16.refs_10_) | copy-start | bytes 1966084
  311.9 31.4 %collective-permute-start.8 = (bf16[160,2048]{1,0:T(8,128)(2,1)}, bf16[160,2048]{1,0:T(8,128)(2,1)}, u32[]{:S(2)}, u32[]{:S(2)}) collective-permute-start(bf16[160,2048]{1,0:T(8,128)(2,1)} %get-tuple-element.72.refs_3_), channel_id=1, source_target_pairs={{0,1},{1,2},{2,3},{3,0},{4,5},{5,6},{6,7},{7,4},{8,9},{9,10},{10,1... | collective-permute-start | bytes 1966088 | tf_op jit(solution)/shard_map/ppermute | solution.py:535
  312.1 42.0 %collective-permute-start.4 = (bf16[160,2048]{1,0:T(8,128)(2,1)}, bf16[160,2048]{1,0:T(8,128)(2,1)}, u32[]{:S(2)}, u32[]{:S(2)}) collective-permute-start(bf16[160,2048]{1,0:T(8,128)(2,1)} %get-tuple-element.68.refs_0_), channel_id=1, source_target_pairs={{0,1},{1,2},{2,3},{3,0},{4,5},{5,6},{6,7},{7,4},{8,9},{9,10},{10,1... | collective-permute-start | bytes 1966088 | tf_op jit(solution)/shard_map/ppermute | solution.py:535
  326.0 29.4 %collective-permute-start.6 = (bf16[160,2048]{1,0:T(8,128)(2,1)}, bf16[160,2048]{1,0:T(8,128)(2,1)S(1)}, u32[]{:S(2)}, u32[]{:S(2)}) collective-permute-start(bf16[160,2048]{1,0:T(8,128)(2,1)} %get-tuple-element.68.refs_0_), channel_id=1, source_target_pairs={{0,3},{1,0},{2,1},{3,2},{4,7},{5,4},{6,5},{7,6},{8,11},{9,8},{10,9... | collective-permute-start | bytes 1966088 | tf_op jit(solution)/shard_map/ppermute | solution.py:536
  326.3 41.7 %collective-permute-start = (bf16[512,640]{1,0:T(8,128)(2,1)}, bf16[512,640]{1,0:T(8,128)(2,1)S(1)}, u32[]{:S(2)}, u32[]{:S(2)}) collective-permute-start(bf16[512,640]{1,0:T(8,128)(2,1)} %get-tuple-element.66.refs_15_), channel_id=1, source_target_pairs={{0,1},{1,2},{2,3},{3,0},{4,5},{5,6},{6,7},{7,4},{8,9},{9,10},{10,1... | collective-permute-start | bytes 1966088 | tf_op jit(solution)/shard_map/ppermute | solution.py:535
  339.8 31.6 %collective-permute-start.2 = (bf16[512,640]{1,0:T(8,128)(2,1)}, bf16[512,640]{1,0:T(8,128)(2,1)S(1)}, u32[]{:S(2)}, u32[]{:S(2)}) collective-permute-start(bf16[512,640]{1,0:T(8,128)(2,1)} %get-tuple-element.66.refs_15_), channel_id=1, source_target_pairs={{0,3},{1,0},{2,1},{3,2},{4,7},{5,4},{6,5},{7,6},{8,11},{9,8},{10,9... | collective-permute-start | bytes 1966088 | tf_op jit(solution)/shard_map/ppermute | solution.py:536
  343.3 38.8 %collective-permute-start.20 = (bf16[512,640]{1,0:T(8,128)(2,1)}, bf16[512,640]{1,0:T(8,128)(2,1)S(1)}, u32[]{:S(2)}, u32[]{:S(2)}) collective-permute-start(bf16[512,640]{1,0:T(8,128)(2,1)} %get-tuple-element.77.refs_12_), channel_id=1, source_target_pairs={{0,1},{1,2},{2,3},{3,0},{4,5},{5,6},{6,7},{7,4},{8,9},{9,10},{10,1... | collective-permute-start | bytes 1966088 | tf_op jit(solution)/shard_map/ppermute | solution.py:535
  354.1 28.3 %collective-permute-start.22 = (bf16[512,640]{1,0:T(8,128)(2,1)}, bf16[512,640]{1,0:T(8,128)(2,1)S(1)}, u32[]{:S(2)}, u32[]{:S(2)}) collective-permute-start(bf16[512,640]{1,0:T(8,128)(2,1)} %get-tuple-element.77.refs_12_), channel_id=1, source_target_pairs={{0,3},{1,0},{2,1},{3,2},{4,7},{5,4},{6,5},{7,6},{8,11},{9,8},{10,9... | collective-permute-start | bytes 1966088 | tf_op jit(solution)/shard_map/ppermute | solution.py:536
  355.4 33.9 %copy-start.1 = (bf16[160,2048]{1,0:T(8,128)(2,1)}, bf16[160,2048]{1,0:T(8,128)(2,1)S(1)}, u32[]{:S(2)}) copy-start(bf16[160,2048]{1,0:T(8,128)(2,1)S(1)} %collective-permute-done.6.refs_2_) | copy-start | bytes 1966084
  355.4 33.7 %collective-permute-start.17 = (bf16[80,2048]{1,0:T(8,128)(2,1)S(1)}, bf16[80,2048]{1,0:T(8,128)(2,1)S(1)}, u32[]{:S(2)}, u32[]{:S(2)}) collective-permute-start(bf16[80,2048]{1,0:T(8,128)(2,1)S(1)} %slice.56), channel_id=1, source_target_pairs={{0,1},{1,2},{2,3},{3,0},{4,5},{5,6},{6,7},{7,4},{8,9},{9,10},{10,1... | collective-permute-start | bytes 983048 | tf_op jit(solution)/shard_map/ppermute | solution.py:546
  368.0 38.4 %copy-start.2 = (bf16[512,640]{1,0:T(8,128)(2,1)}, bf16[512,640]{1,0:T(8,128)(2,1)S(1)}, u32[]{:S(2)}) copy-start(bf16[512,640]{1,0:T(8,128)(2,1)S(1)} %collective-permute-done.refs_16_) | copy-start | bytes 1966084
  368.0 21.1 %collective-permute-start.19 = (bf16[80,2048]{1,0:T(8,128)(2,1)S(1)}, bf16[80,2048]{1,0:T(8,128)(2,1)S(1)}, u32[]{:S(2)}, u32[]{:S(2)}) collective-permute-start(bf16[80,2048]{1,0:T(8,128)(2,1)S(1)} %slice.57), channel_id=1, source_target_pairs={{0,3},{1,0},{2,1},{3,2},{4,7},{5,4},{6,5},{7,6},{8,11},{9,8},{10,9... | collective-permute-start | bytes 983048 | tf_op jit(solution)/shard_map/ppermute | solution.py:547
  371.3 35.8 %copy-start.3 = (bf16[512,640]{1,0:T(8,128)(2,1)}, bf16[512,640]{1,0:T(8,128)(2,1)S(1)}, u32[]{:S(2)}) copy-start(bf16[512,640]{1,0:T(8,128)(2,1)S(1)} %collective-permute-done.2.refs_17_) | copy-start | bytes 1966084
  371.3 24.8 %collective-permute-start.13 = (bf16[80,2048]{1,0:T(8,128)(2,1)S(1)}, bf16[80,2048]{1,0:T(8,128)(2,1)S(1)}, u32[]{:S(2)}, u32[]{:S(2)}) collective-permute-start(bf16[80,2048]{1,0:T(8,128)(2,1)S(1)} %slice.54), channel_id=1, source_target_pairs={{0,1},{1,2},{2,3},{3,0},{4,5},{5,6},{6,7},{7,4},{8,9},{9,10},{10,1... | collective-permute-start | bytes 983048 | tf_op jit(solution)/shard_map/ppermute | solution.py:546
  382.1 25.1 %copy-start.4 = (bf16[512,640]{1,0:T(8,128)(2,1)}, bf16[512,640]{1,0:T(8,128)(2,1)S(1)}, u32[]{:S(2)}) copy-start(bf16[512,640]{1,0:T(8,128)(2,1)S(1)} %collective-permute-done.20.refs_13_) | copy-start | bytes 1966084
  382.1 14.3 %collective-permute-start.15 = (bf16[80,2048]{1,0:T(8,128)(2,1)S(1)}, bf16[80,2048]{1,0:T(8,128)(2,1)S(1)}, u32[]{:S(2)}, u32[]{:S(2)}) collective-permute-start(bf16[80,2048]{1,0:T(8,128)(2,1)S(1)} %slice.55), channel_id=1, source_target_pairs={{0,3},{1,0},{2,1},{3,2},{4,7},{5,4},{6,5},{7,6},{8,11},{9,8},{10,9... | collective-permute-start | bytes 983048 | tf_op jit(solution)/shard_map/ppermute | solution.py:547
  382.4 24.8 %copy-start.5 = (bf16[512,640]{1,0:T(8,128)(2,1)}, bf16[512,640]{1,0:T(8,128)(2,1)S(1)}, u32[]{:S(2)}) copy-start(bf16[512,640]{1,0:T(8,128)(2,1)S(1)} %collective-permute-done.22.refs_14_) | copy-start | bytes 1966084
  382.4 20.5 %collective-permute-start.11 = (bf16[80,2048]{1,0:T(8,128)(2,1)S(1)}, bf16[80,2048]{1,0:T(8,128)(2,1)S(1)}, u32[]{:S(2)}, u32[]{:S(2)}) collective-permute-start(bf16[80,2048]{1,0:T(8,128)(2,1)S(1)} %slice.53), channel_id=1, source_target_pairs={{0,3},{1,0},{2,1},{3,2},{4,7},{5,4},{6,5},{7,6},{8,11},{9,8},{10,9... | collective-permute-start | bytes 983048 | tf_op jit(solution)/shard_map/ppermute | solution.py:547
  389.1 21.1 %copy-start.6 = (bf16[80,2048]{1,0:T(8,128)(2,1)}, bf16[80,2048]{1,0:T(8,128)(2,1)S(1)}, u32[]{:S(2)}) copy-start(bf16[80,2048]{1,0:T(8,128)(2,1)S(1)} %collective-permute-done.17.refs_6_) | copy-start | bytes 983044
  389.1 18.1 %collective-permute-start.9 = (bf16[80,2048]{1,0:T(8,128)(2,1)S(1)}, bf16[80,2048]{1,0:T(8,128)(2,1)S(1)}, u32[]{:S(2)}, u32[]{:S(2)}) collective-permute-start(bf16[80,2048]{1,0:T(8,128)(2,1)S(1)} %slice.52), channel_id=1, source_target_pairs={{0,1},{1,2},{2,3},{3,0},{4,5},{5,6},{6,7},{7,4},{8,9},{9,10},{10,1... | collective-permute-start | bytes 983048 | tf_op jit(solution)/shard_map/ppermute | solution.py:546
  389.1 21.1 %copy-start.7 = (bf16[80,2048]{1,0:T(8,128)(2,1)}, bf16[80,2048]{1,0:T(8,128)(2,1)S(1)}, u32[]{:S(2)}) copy-start(bf16[80,2048]{1,0:T(8,128)(2,1)S(1)} %collective-permute-done.19.refs_7_) | copy-start | bytes 983044
  389.1 21.0 %collective-permute-start.5 = (bf16[80,2048]{1,0:T(8,128)(2,1)S(1)}, bf16[80,2048]{1,0:T(8,128)(2,1)S(1)}, u32[]{:S(2)}, u32[]{:S(2)}) collective-permute-start(bf16[80,2048]{1,0:T(8,128)(2,1)S(1)} %slice.50), channel_id=1, source_target_pairs={{0,1},{1,2},{2,3},{3,0},{4,5},{5,6},{6,7},{7,4},{8,9},{9,10},{10,1... | collective-permute-start | bytes 983048 | tf_op jit(solution)/shard_map/ppermute | solution.py:546
  396.1 24.1 %collective-permute-start.7 = (bf16[80,2048]{1,0:T(8,128)(2,1)}, bf16[80,2048]{1,0:T(8,128)(2,1)}, u32[]{:S(2)}, u32[]{:S(2)}) collective-permute-start(bf16[80,2048]{1,0:T(8,128)(2,1)} %slice.51), channel_id=1, source_target_pairs={{0,3},{1,0},{2,1},{3,2},{4,7},{5,4},{6,5},{7,6},{8,11},{9,8},{10,9... | collective-permute-start | bytes 983048 | tf_op jit(solution)/shard_map/ppermute | solution.py:547
  396.4 23.8 %collective-permute-start.21 = (bf16[256,640]{1,0:T(8,128)(2,1)S(1)}, bf16[256,640]{1,0:T(8,128)(2,1)}, u32[]{:S(2)}, u32[]{:S(2)}) collective-permute-start(bf16[256,640]{1,0:T(8,128)(2,1)S(1)} %slice.58), channel_id=1, source_target_pairs={{0,1},{1,2},{2,3},{3,0},{4,5},{5,6},{6,7},{7,4},{8,9},{9,10},{10,1... | collective-permute-start | bytes 983048 | tf_op jit(solution)/shard_map/ppermute | solution.py:546
  402.8 17.4 %collective-permute-start.23 = (bf16[256,640]{1,0:T(8,128)(2,1)S(1)}, bf16[256,640]{1,0:T(8,128)(2,1)}, u32[]{:S(2)}, u32[]{:S(2)}) collective-permute-start(bf16[256,640]{1,0:T(8,128)(2,1)S(1)} %slice.59), channel_id=1, source_target_pairs={{0,3},{1,0},{2,1},{3,2},{4,7},{5,4},{6,5},{7,6},{8,11},{9,8},{10,9... | collective-permute-start | bytes 983048 | tf_op jit(solution)/shard_map/ppermute | solution.py:547
  407.2 16.6 %collective-permute-start.1 = (bf16[256,640]{1,0:T(8,128)(2,1)}, bf16[256,640]{1,0:T(8,128)(2,1)}, u32[]{:S(2)}, u32[]{:S(2)}) collective-permute-start(bf16[256,640]{1,0:T(8,128)(2,1)} %slice.48), channel_id=1, source_target_pairs={{0,1},{1,2},{2,3},{3,0},{4,5},{5,6},{6,7},{7,4},{8,9},{9,10},{10,1... | collective-permute-start | bytes 983048 | tf_op jit(solution)/shard_map/ppermute | solution.py:546
  410.9 12.9 %collective-permute-start.3 = (bf16[256,640]{1,0:T(8,128)(2,1)S(1)}, bf16[256,640]{1,0:T(8,128)(2,1)}, u32[]{:S(2)}, u32[]{:S(2)}) collective-permute-start(bf16[256,640]{1,0:T(8,128)(2,1)S(1)} %slice.49), channel_id=1, source_target_pairs={{0,3},{1,0},{2,1},{3,2},{4,7},{5,4},{6,5},{7,6},{8,11},{9,8},{10,9... | collective-permute-start | bytes 983048 | tf_op jit(solution)/shard_map/ppermute | solution.py:547
  (5 other events, 38.9 us)
